TPU v7x, 128 devices: a whole 4x4x4 slice. The times are simulated.
128 devices in a mesh: blk: 16 (over z_lo, y, core), seq: 8 (over x, z_hi).
Axes of the slice: x: 4, y: 4, z: 4 (z_hi: 2, z_lo: 2; z = z_hi * 2 + z_lo), core: 2. Of those that a mesh axis runs over, the one named last changes fastest.
Arguments:
- layer_input: bfloat16 [16, 1024, 8192], P('blk', 'seq'), may hold values from -6 to 6
- queries: bfloat16 [16, 1024, 4096], P('blk', 'seq'), may hold values from -48 to 48, as said below
- grad_out: bfloat16 [16, 1024, 4096], P('blk', 'seq'), may hold values from -6 to 6
- segment_ids: int32 [16, 1024], P('blk', 'seq'), may hold values from 0 to 3, never falling along the last dimension, each value on 1 to 512 neighbouring positions
- kv_weight: bfloat16 [8192, 1024], P(('blk', 'seq')), may hold values from -0.0625 to 0.0625
- norm_gain: float32 [8192], replicated, may hold values from 0.5 to 1.5
Outputs:
- attended: bfloat16 [16, 1024, 4096], P('blk', 'seq')
- grad_queries: bfloat16 [16, 1024, 4096], P('blk', 'seq')
- grad_input: bfloat16 [16, 1024, 8192], P('blk', 'seq')
- grad_weight: float32 [8192, 1024], P(('blk', 'seq'))
- grad_gain: float32 [8192], replicated
Inputs may be any that keep to these rules, and one draw needn't show every extreme that they name: Projected queries; some rows may be larger than others.
All inputs are finite; a program needn't handle non-finite values.
Results may differ from a plain program's by a relative error of at most 0.02.
The roundings to bfloat16 on the way count: a program that leaves them out, or rounds other values in their place, can miss the bound.
Values may be sent and summed in bfloat16 or wider, within the bound.
No kernel may reach another device: no remote copies, remote signals or barrier semaphores. Data moves between devices by JAX's collectives and lax.ppermute only.
A program may use at most 128 MiB of HBM per device.

v0:
```python
import jax
import jax.numpy as jnp
from jax import lax
from jax.sharding import PartitionSpec as P

HEAD = 128
epsilon = 1e-05


def cut_along(shard, dim, length):
    lengths = shard.shape
    pieces = shard.reshape(*lengths[:dim], length, lengths[dim] // length, *lengths[dim + 1 :])
    return jnp.moveaxis(pieces, dim, 0)


def sum_at_owner(shard, axis, dim):
    length = lax.axis_size(axis)
    pieces = lax.all_to_all(cut_along(shard, dim, length), axis, 0, 0, tiled=True)
    return jnp.sum(pieces, axis=0)


def shards(layer_input, queries, grad_out, segment_ids, kv_weight, norm_gain):
    f32 = jnp.float32
    tok_rows = layer_input.shape[1]
    model_width = layer_input.shape[2]
    seq_devices = lax.axis_size("seq")
    blk_devices = lax.axis_size("blk")
    length = tok_rows * seq_devices
    seq_index = lax.axis_index("seq")
    kv_total = kv_weight.shape[1]
    kv_width = kv_total // 2
    kv_heads = kv_width // HEAD
    query_count = queries.shape[2] // HEAD
    group_size = query_count // kv_heads
    score_scale = HEAD ** (-0.5)
    piece_cols = kv_weight.shape[0]
    source = layer_input[0].astype(f32)
    inv_rms = lax.rsqrt(jnp.mean(source * source, axis=1, keepdims=True) + epsilon)
    scaled = source * inv_rms
    normed = (scaled * norm_gain).astype(jnp.bfloat16)
    split_cols = normed.reshape(tok_rows, blk_devices, seq_devices, piece_cols)
    columns = lax.all_to_all(split_cols, "seq", split_axis=2, concat_axis=0, tiled=True).reshape(
        length, blk_devices * piece_cols
    )
    weight_slab = lax.all_gather(kv_weight, "blk", axis=0, tiled=True)
    query_heads = queries[0].reshape(tok_rows, kv_heads, group_size, HEAD)
    query_pos = seq_index * tok_rows + jnp.arange(tok_rows, dtype=jnp.int32)
    query_doc = segment_ids[0]
    grad_heads = grad_out[0].reshape(tok_rows, kv_heads, group_size, HEAD).transpose(1, 2, 0, 3)

    def scores_of(kv_piece, doc_piece):
        rows_here = kv_piece.shape[0]
        key_heads = kv_piece[:, :kv_width].reshape(rows_here, kv_heads, HEAD)
        raw_scores = (
            jnp.einsum("qgjd,kgd->gjqk", query_heads, key_heads, preferred_element_type=f32)
            * score_scale
        )
        key_pos = jnp.arange(rows_here, dtype=jnp.int32)
        allowed = (key_pos[None, :] <= query_pos[:, None]) & (
            doc_piece[None, :] == query_doc[:, None]
        )
        return (jnp.where(allowed, raw_scores, -1e30), allowed, key_heads)

    stat_shape = (kv_heads, group_size, tok_rows, 1)
    kv_own = sum_at_owner(
        jnp.dot(columns, weight_slab, preferred_element_type=f32), "seq", 0
    ).astype(jnp.bfloat16)
    row_max = jnp.full(stat_shape, -1e30, f32)
    kv_piece = lax.all_gather(kv_own, "seq", axis=0, tiled=True)
    doc_piece = lax.all_gather(query_doc, "seq", axis=0, tiled=True)
    rows_here = kv_piece.shape[0]
    masked, allowed, key_heads = scores_of(kv_piece, doc_piece)
    new_max = jnp.maximum(row_max, jnp.max(masked, axis=-1, keepdims=True))
    expo_terms = jnp.where(allowed, jnp.exp(masked - new_max), 0.0)
    value_heads = kv_piece[:, kv_width:].reshape(rows_here, kv_heads, HEAD)
    weights = expo_terms.astype(jnp.bfloat16)
    weighted = jnp.einsum("gjqk,kgd->gjqd", weights, value_heads, preferred_element_type=f32)
    row_sum = jnp.sum(expo_terms, axis=-1, keepdims=True)
    row_max, row_sum, weighted = (new_max, row_sum, weighted)
    summed = weighted / row_sum
    attended = (
        summed.transpose(2, 0, 1, 3).reshape(tok_rows, query_count * HEAD).astype(jnp.bfloat16)
    )
    log_total = row_max + jnp.log(row_sum)
    attended_heads = attended.reshape(tok_rows, kv_heads, group_size, HEAD).transpose(1, 2, 0, 3)
    row_delta = jnp.sum(grad_heads.astype(f32) * attended_heads.astype(f32), axis=-1, keepdims=True)
    kv_piece = lax.all_gather(kv_own, "seq", axis=0, tiled=True)
    doc_piece = lax.all_gather(query_doc, "seq", axis=0, tiled=True)
    rows_here = kv_piece.shape[0]
    masked, allowed, key_heads = scores_of(kv_piece, doc_piece)
    softmax_probs = jnp.where(allowed, jnp.exp(masked - log_total), 0.0)
    value_heads = kv_piece[:, kv_width:].reshape(rows_here, kv_heads, HEAD)
    grad_probs = jnp.einsum("gjqd,kgd->gjqk", grad_heads, value_heads, preferred_element_type=f32)
    grad_scores = (softmax_probs * (grad_probs - row_delta)).astype(jnp.bfloat16)
    probs_half = softmax_probs.astype(jnp.bfloat16)
    grad_values = jnp.einsum("gjqk,gjqd->kgd", probs_half, grad_heads, preferred_element_type=f32)
    grad_keys = (
        jnp.einsum("gjqk,qgjd->kgd", grad_scores, query_heads, preferred_element_type=f32)
        * score_scale
    )
    grad_query = (
        jnp.einsum("gjqk,kgd->qgjd", grad_scores, key_heads, preferred_element_type=f32)
        * score_scale
    )
    new_rows = jnp.concatenate(
        [grad_keys.reshape(rows_here, kv_width), grad_values.reshape(rows_here, kv_width)], axis=1
    )
    grad_rows = new_rows
    grad_query, grad_rows = (grad_query, grad_rows)
    grad_own = sum_at_owner(grad_rows, "seq", 0).astype(jnp.bfloat16)
    grad_kv = lax.all_gather(grad_own, "seq", axis=0, tiled=True)
    grad_queries = grad_query.reshape(tok_rows, query_count * HEAD).astype(jnp.bfloat16)
    slab_back = lax.all_gather(kv_weight, "blk", axis=0, tiled=True)
    grad_weight = lax.psum_scatter(
        lax.dot_general(columns, grad_kv, (((0,), (0,)), ((), ())), preferred_element_type=f32),
        "blk",
        scatter_dimension=0,
        tiled=True,
    )
    grad_cols = lax.dot_general(
        grad_kv, slab_back, (((1,), (1,)), ((), ())), preferred_element_type=f32
    ).astype(jnp.bfloat16)
    grad_cols = grad_cols.reshape(length, blk_devices, 1, piece_cols)
    grad_normed = lax.all_to_all(grad_cols, "seq", split_axis=0, concat_axis=2, tiled=True).reshape(
        tok_rows, model_width
    )
    grad_norm = grad_normed.astype(f32)
    grad_gain = lax.psum(jnp.sum(grad_norm * scaled, axis=0), ("blk", "seq"))
    grad_hat = grad_norm * norm_gain
    grad_input = inv_rms * (grad_hat - scaled * jnp.mean(grad_hat * scaled, axis=1, keepdims=True))
    return (
        attended[None],
        grad_queries[None],
        grad_input.astype(jnp.bfloat16)[None],
        grad_weight,
        grad_gain,
    )


def solution(mesh):
    in_specs = (
        P("blk", "seq", None),
        P("blk", "seq", None),
        P("blk", "seq", None),
        P("blk", "seq"),
        P(("blk", "seq"), None),
        P(),
    )
    out_specs = (
        P("blk", "seq", None),
        P("blk", "seq", None),
        P("blk", "seq", None),
        P(("blk", "seq"), None),
        P(),
    )
    return jax.shard_map(shards, mesh=mesh, in_specs=in_specs, out_specs=out_specs, check_vma=False)
```

profile of v0, /device:TPU:1, one launch (start us, length us, event | category | flops | bytes accessed | tf_op | source)
XLA Modules:
  0.0 534.6 jit_solution(473694179402004484)
XLA Ops:
  8.0 3.2 copy.148
  17.7 38.3 %all_to_all.34 = bf16[128,16,8,64]{0,3,1,2:T(8,128)(2,1)} all-to-all(bf16[128,16,8,64]{0,3,1,2:T(8,128)(2,1)S(1)} %copy.149), channel_id=1, replica_groups=mesh['blk'=16,'seq'=8] {'seq'}, dimensions={2} | all-to-all | bytes 4194304 | tf_op jit(solution)/shard_map/all_to_all | solution.py:42
  56.0 8.3 %all-gather.5.cloned.1.call-done = bf16[1024,1024]{1,0:T(8,128)(2,1)} async-done(((bf16[64,1024]{1,0:T(8,128)(2,1)}), bf16[1024,1024]{1,0:T(8,128)(2,1)}) %all-gather.5.cloned.1.call-update) | async-done | bytes 2097168 | tf_op jit(solution)/shard_map/all_gather | solution.py:45
  64.3 4.6 fusion.22
  68.9 55.1 %all_to_all.35 = f32[8,128,1024]{2,1,0:T(8,128)} all-to-all(f32[8,128,1024]{2,1,0:T(8,128)S(1)} %fusion.22), channel_id=1, replica_groups=mesh['blk'=16,'seq'=8] {'seq'}, dimensions={0} | all-to-all | bytes 8388608 | tf_op jit(solution)/shard_map/all_to_all | solution.py:18
  124.1 3.4 reduce_sum.66
  131.0 17.1 %all-gather = s32[1,1024]{1,0:T(1,128)S(1)} all-gather(s32[1,128]{1,0:T(1,128)S(1)} %copy-done.8), channel_id=2, replica_groups=mesh['blk'=16,'seq'=8] {'seq'}, dimensions={1}, use_global_device_ids=true | all-gather | bytes 4608 | tf_op jit(solution)/shard_map/all_gather | solution.py:70
  148.4 30.2 %all-gather.7.cloned.1.call-done = bf16[1024,1024]{1,0:T(8,128)(2,1)} async-done(((bf16[128,1024]{1,0:T(8,128)(2,1)}), bf16[1024,1024]{1,0:T(8,128)(2,1)}) %all-gather.7.cloned.1.call-update) | async-done | bytes 2097168 | tf_op jit(solution)/shard_map/all_gather | solution.py:69
  183.0 9.1 %fusion.33 = (f32[4,8,128]{2,1,0:T(8,128)S(1)}, f32[4,8,128,1024]{2,3,1,0:T(8,128)}) fusion(bf16[1024,4,128,1]{0,2,3,1:T(8,128)(2,1)S(1)} %bitcast.122, bf16[128,4,8,128]{3,2,1,0:T(8,128)(2,1)} %bitcast.124, pred[128,1024]{0,1:T(8,128)(4,1)S(1)} %fusion.29), kind=kOutput, calls=%fused_computation.52 | convolution fusion | flops 1086320640 | bytes 19021824 | tf_op jit(solution)/shard_map/qgjd,kgd->gjqk/dot_general | solution.py:55
  194.4 8.7 %fusion.1 = f32[4,8,128]{2,1,0:T(8,128)S(1)} fusion(f32[4,8,128,1024]{2,3,1,0:T(8,128)} %get-tuple-element.45, f32[4,8,128]{2,1,0:T(8,128)S(1)} %broadcast_maximum_fusion, pred[128,1024]{0,1:T(8,128)(4,1)S(1)} %fusion.29), kind=kLoop, calls=%fused_computation.5 | loop fusion | flops 12578816 | bytes 16941056 | tf_op jit(solution)/shard_map/reduce_sum | solution.py:78
  203.1 9.9 %fusion.21 = (bf16[128,4,8,128]{0,3,2,1:T(8,128)(2,1)}, f32[4,8,128,128]{2,3,1,0:T(8,128)S(1)}) fusion(f32[128,4,8]{0,2,1:T(8,128)S(1)} %bitcast.140, bf16[1024,4,128,1]{0,2,3,1:T(8,128)(2,1)S(1)} %bitcast.138, f32[4,8,128,1024]{2,3,1,0:T(8,128)} %get-tuple-element.45, f32[4,8,128]{2,1,0:T(8,128)S(1)} %broadcast_maximum_fusion, ...), kind=kOutput, calls=%fused_computation.32 | convolution fusion | flops 1087373312 | bytes 21135360 | tf_op jit(solution)/shard_map/gjqk,kgd->gjqd/dot_general | solution.py:77
  213.4 9.5 %fusion.24 = f32[1024,4,128]{2,0,1:T(8,128)} fusion(bf16[4,8,128,128]{2,3,1,0:T(8,128)(2,1)S(1)} %bitcast.131, f32[4,8,128,1024]{2,3,1,0:T(8,128)} %get-tuple-element.45, f32[4,8,128]{2,1,0:T(8,128)S(1)} %log_add_fusion, pred[128,1024]{0,1:T(8,128)(4,1)S(1)} %fusion.29), kind=kOutput, calls=%fused_computation.39 | convolution fusion | flops 1086324736 | bytes 20070400 | tf_op jit(solution)/shard_map/gjqk,gjqd->kgd/dot_general | solution.py:96
  222.9 10.9 %fusion = bf16[4,8,128,1024]{2,3,1,0:T(8,128)(2,1)} fusion(f32[4,8,128,1024]{2,3,1,0:T(8,128)} %get-tuple-element.45, bf16[1024,4,128,1]{0,2,3,1:T(8,128)(2,1)S(1)} %bitcast.139, bf16[4,8,128,128]{2,3,1,0:T(8,128)(2,1)S(1)} %bitcast.132, f32[4,8,128]{2,1,0:T(8,128)S(1)} %multiply_reduce_fusion.3, f32[4,8,128]{2,1,0:T(8,128)S(1)} %log_add_fusion, ...), kind=kOutput, calls=%fused_computation.1 | convolution fusion | flops 1094713344 | bytes 27426816 | tf_op jit(solution)/shard_map/gjqd,kgd->gjqk/dot_general | solution.py:93
  236.7 3.5 copy.194
  240.2 7.1 %fusion.20 = f32[1024,4,128]{2,0,1:T(8,128)} fusion(bf16[4,8,128,1024]{2,3,1,0:T(8,128)(2,1)} %fusion, bf16[128,4,8,128]{3,2,1,0:T(8,128)(2,1)S(1)} %bitcast.125), kind=kOutput, calls=%fused_computation.30 | convolution fusion | flops 1074266112 | bytes 11534336 | tf_op jit(solution)/shard_map/gjqk,qgjd->kgd/dot_general | solution.py:98
  253.5 50.9 %all_to_all.36 = f32[8,128,1024]{1,2,0:T(8,128)} all-to-all(f32[8,128,1024]{1,2,0:T(8,128)S(1)} %copy.164), channel_id=1, replica_groups=mesh['blk'=16,'seq'=8] {'seq'}, dimensions={0} | all-to-all | bytes 8388608 | tf_op jit(solution)/shard_map/all_to_all | solution.py:18
  304.4 3.2 reduce_sum.69
  307.8 4.7 copy.171
  312.5 51.4 %all-gather.9.cloned.1.call-done = bf16[1024,1024]{0,1:T(8,128)(2,1)} async-done(((bf16[128,1024]{0,1:T(8,128)(2,1)}), bf16[1024,1024]{0,1:T(8,128)(2,1)}) %all-gather.9.cloned.1.call-update) | async-done | bytes 2097168 | tf_op jit(solution)/shard_map/all_gather | solution.py:111
  363.9 6.5 %fusion.17 = f32[1024,1024]{1,0:T(8,128)} fusion(bf16[1024,1024]{0,1:T(8,128)(2,1)} %all-gather.9.cloned.1.call-done, bf16[128,8,8,128]{3,2,1,0:T(8,128)(2,1)} %bitcast.135), kind=kOutput, calls=%fused_computation.26 | convolution fusion | flops 2147483648 | bytes 8388608 | tf_op jit(solution)/shard_map/dot_general | solution.py:115
  370.4 5.9 %convolution_convert_fusion = bf16[1024,1024]{0,1:T(8,128)(2,1)} fusion(bf16[1024,1024]{1,0:T(8,128)(2,1)} %all-gather.5.cloned.1.call-done, bf16[1024,1024]{0,1:T(8,128)(2,1)} %all-gather.9.cloned.1.call-done), kind=kOutput, calls=%fused_computation.38 | convolution fusion | flops 2148532224 | bytes 6291456 | tf_op jit(solution)/shard_map/dot_general | solution.py:120
  376.3 6.2 %copy.166 = bf16[1024,16,1,64]{3,1,2,0:T(8,128)(2,1)} copy(bf16[1024,16,1,64]{0,3,1,2:T(8,128)(2,1)} %bitcast.134) | data formatting | bytes 4194304 | tf_op jit(solution)/shard_map/reshape | solution.py:123
  382.5 7.6 %reshape.223 = bf16[8,2,65536]{2,1,0:T(2,128)(2,1)} reshape(bf16[1024,1,16,64]{3,2,1,0:T(8,128)(2,1)} %bitcast.119) | data formatting | bytes 4194304
  390.1 4.6 all-to-all-start.3
  397.9 5.6 %multiply_convert_fusion.1 = bf16[4,128,8,128]{3,1,2,0:T(8,128)(2,1)} fusion(bf16[1024,4,128,1]{0,2,3,1:T(8,128)(2,1)S(1)} %bitcast.123, bf16[4,8,128,1024]{2,3,1,0:T(8,128)(2,1)} %fusion), kind=kOutput, calls=%fused_computation.35 | convolution fusion | flops 1074790400 | bytes 10485760 | tf_op jit(solution)/shard_map/gjqk,kgd->qgjd/dot_general | solution.py:102
  405.9 22.6 %all-to-all-done.3 = bf16[8,2,65536]{2,1,0:T(2,128)(2,1)} async-done(((bf16[8,2,65536]{2,1,0:T(2,128)(2,1)}), bf16[8,2,65536]{2,1,0:T(2,128)(2,1)}, u32[]{:S(2)}, u32[]{:S(2)}) %all-to-all-start.3) | async-done | bytes 2097184 | tf_op jit(solution)/shard_map/all_to_all | solution.py:124
  428.4 7.4 %reshape.224 = bf16[1024,1,16,64]{3,2,1,0:T(8,128)(2,1)} reshape(bf16[8,2,65536]{2,1,0:T(2,128)(2,1)} %all-to-all-done.3) | data formatting | bytes 4194304
  435.8 5.5 %copy.167 = bf16[1024,16,1,64]{0,3,2,1:T(8,128)(2,1)} copy(bf16[1024,16,1,64]{3,1,2,0:T(8,128)(2,1)} %bitcast.120) | data formatting | bytes 4194304 | tf_op jit(solution)/shard_map/all_to_all | solution.py:124
  446.7 4.8 multiply_reduce_fusion
  451.5 4.4 fusion.16
  455.9 4.1 copy.175
  460.2 67.6 %psum.7 = f32[8192]{0:T(1024)} all-reduce(f32[8192]{0:T(1024)S(1)} %reduce_sum.72), channel_id=1, replica_groups=mesh['blk'=16,'seq'=8] {'blk','seq'}, use_global_device_ids=true, to_apply=%region_9.10 | all-reduce | flops 8192 | bytes 65536 | tf_op jit(solution)/shard_map/psum | solution.py:128
  (57 shorter events, 38.8 us)
Async XLA Ops:
  7.2 57.1 %all-gather.5.cloned.1.call-start = ((), (), s32[]{:S(2)}) async-start(), calls=%async_computation.5 | async-start | bytes 2228224 | tf_op jit(solution)/shard_map/all_gather | solution.py:45
  7.9 5.5 %copy-start.7 = (f32[8192]{0:T(1024)S(1)}, f32[8192]{0:T(1024)}, u32[]{:S(2)}) copy-start(f32[8192]{0:T(1024)} %param.11) | copy-start | bytes 98308
  7.9 170.6 %all-gather.7.cloned.1.call-start = ((), (), s32[]{:S(2)}) async-start(), calls=%async_computation.6 | async-start | bytes 2359296 | tf_op jit(solution)/shard_map/all_gather | solution.py:69
  124.0 3.5 copy-start.5
  124.0 7.0 %copy-start.8 = (s32[1,128]{1,0:T(1,128)S(1)}, s32[1,128]{1,0:T(1,128)}, u32[]{:S(2)}) copy-start(s32[1,128]{1,0:T(1,128)} %param.9) | copy-start | bytes 1540
  127.5 236.4 %all-gather.9.cloned.1.call-start = ((), (), s32[]{:S(2)}) async-start(), calls=%async_computation.7 | async-start | bytes 2359296 | tf_op jit(solution)/shard_map/all_gather | solution.py:111
  194.4 8.7 %copy-start.6 = (bf16[1024,512]{0,1:T(8,128)(2,1)S(1)}, bf16[1024,512]{0,1:T(8,128)(2,1)}, u32[]{:S(2)}) copy-start(bf16[1024,512]{0,1:T(8,128)(2,1)} %copy.154) | copy-start | bytes 3145732
  203.1 9.9 %copy-start.3 = (bf16[1,128,4096]{1,2,0:T(8,128)(2,1)S(1)}, bf16[1,128,4096]{1,2,0:T(8,128)(2,1)}, u32[]{:S(2)}) copy-start(bf16[1,128,4096]{1,2,0:T(8,128)(2,1)} %copy.156) | copy-start | bytes 3145732
  236.7 3.5 copy-start.1
  250.2 2.2 copy-start.2
  307.6 220.3 %reduce-scatter.2.cloned.1.call-start = ((), (), s32[]{:S(2)}) async-start(), calls=%async_computation.8 | async-start | bytes 4456448 | tf_op jit(solution)/shard_map/reduce_scatter | solution.py:114
  390.1 38.4 %all-to-all-start.3 = ((bf16[8,2,65536]{2,1,0:T(2,128)(2,1)}), bf16[8,2,65536]{2,1,0:T(2,128)(2,1)}, u32[]{:S(2)}, u32[]{:S(2)}) async-start(bf16[8,2,65536]{2,1,0:T(2,128)(2,1)} %reshape.223), calls=%async_computation.3 | async-start | bytes 4194304 | tf_op jit(solution)/shard_map/all_to_all | solution.py:124
  444.4 2.2 copy-start
  444.4 2.3 copy-start.4
Sparse Core Ops, SparseCore 0:
  9.7 54.5 all-gather.4
  127.6 50.8 all-gather.6
  307.7 56.0 all-gather.8
  370.5 72.2 reduce-scatter.1
where the time goes:
time: 540 us; the launch traced here: 535 us
  blocking collectives  229 us (42%)
  waiting for transfers between devices  113 us (21%)
  local copies, waits for them, and re-layouts  70.6 us (13%)
  matrix products  69.1 us (13%)
  other arithmetic  33.7 us (6%)
  between operations  14.2 us (3%)
    all_to_all x2, blocking collectives, sum_at_owner(): lax.all_to_all(cut_along(shard, dim, length), axis, 0, 0, tiled=True)  106 us
    psum x1, blocking collectives, shards(): grad_gain = lax.psum(jnp.sum(grad_norm * scaled, axis=0), ('blk', 'seq'))  67.6 us
    all_gather x1, waiting for transfers between devices, shards(): grad_kv = lax.all_gather(grad_own, 'seq', axis=0, tiled=True)  51.4 us
    unnamed x29, local copies, waits for them, and re-layouts  38.6 us
    all_to_all x1, blocking collectives, shards(): lax.all_to_all(split_cols, 'seq', split_axis=2, concat_axis=0, tiled=True)  38.3 us
    all_gather x1, waiting for transfers between devices, shards(): kv_piece = lax.all_gather(kv_own, 'seq', axis=0, tiled=True)  30.2 us
    all_to_all x1, waiting for transfers between devices, shards(): lax.all_to_all(grad_cols, 'seq', split_axis=0, concat_axis=2, tiled=True)  22.6 us
    all_gather x1, blocking collectives, shards(): doc_piece = lax.all_gather(query_doc, 'seq', axis=0, tiled=True)  17.1 us
  transfers between devices with their start and end apart: 5, of which 4 were waited for; matrix products, arithmetic and copies ran while one was open for 15% of the time, Pallas kernels for 0%

commit v1 on v0

--- a/solution.py
+++ b/solution.py
@@ -108,7 +108,8 @@
     grad_rows = new_rows
     grad_query, grad_rows = (grad_query, grad_rows)
     grad_own = sum_at_owner(grad_rows, "seq", 0).astype(jnp.bfloat16)
-    grad_kv = lax.all_gather(grad_own, "seq", axis=0, tiled=True)
+    sent = jnp.stack([grad_own] * lax.axis_size("seq"))
+    grad_kv = jnp.concatenate(lax.all_to_all(sent, "seq", 0, 0), axis=0)
     grad_queries = grad_query.reshape(tok_rows, query_count * HEAD).astype(jnp.bfloat16)
     slab_back = lax.all_gather(kv_weight, "blk", axis=0, tiled=True)
     grad_weight = lax.psum_scatter(

time: 540 us -> 519 us (0.961)
  waiting for transfers between devices: 113 us -> 84.7 us
    all_gather x1 -> x0, waiting for transfers between devices: 51.4 us -> none  [shards(): grad_kv = lax.all_gather(grad_own, 'seq', axis=0, tiled=True)]
    all_to_all x0 -> x1, waiting for transfers between devices: none -> 22.8 us  [shards(): grad_kv = jnp.concatenate(lax.all_to_all(sent, 'seq', 0, 0), axis=0)]
where the time goes in v1:
time: 519 us; the launch traced here: 513 us
  blocking collectives  229 us (44%)
  waiting for transfers between devices  84.7 us (16%)
  local copies, waits for them, and re-layouts  74 us (14%)
  matrix products  69.1 us (13%)
  other arithmetic  32.9 us (6%)
  between operations  14.2 us (3%)
  starting transfers between devices  9.2 us (2%)
    all_to_all x2, blocking collectives, sum_at_owner(): lax.all_to_all(cut_along(shard, dim, length), axis, 0, 0, tiled=True)  106 us
    psum x1, blocking collectives, shards(): grad_gain = lax.psum(jnp.sum(grad_norm * scaled, axis=0), ('blk', 'seq'))  67.3 us
    unnamed x29, local copies, waits for them, and re-layouts  38.6 us
    all_to_all x1, blocking collectives, shards(): lax.all_to_all(split_cols, 'seq', split_axis=2, concat_axis=0, tiled=True)  38.3 us
    all_gather x1, waiting for transfers between devices, shards(): kv_piece = lax.all_gather(kv_own, 'seq', axis=0, tiled=True)  30.2 us
    all_to_all x1, waiting for transfers between devices, shards(): grad_kv = jnp.concatenate(lax.all_to_all(sent, 'seq', 0, 0), axis=0)  22.8 us
    all_to_all x1, waiting for transfers between devices, shards(): lax.all_to_all(grad_cols, 'seq', split_axis=0, concat_axis=2, tiled=True)  22.7 us
    all_gather x1, blocking collectives, shards(): doc_piece = lax.all_gather(query_doc, 'seq', axis=0, tiled=True)  17.1 us
  transfers between devices with their start and end apart: 5, of which 4 were waited for; matrix products, arithmetic and copies ran while one was open for 15% of the time, Pallas kernels for 0%

profile of v1, /device:TPU:1, one launch (start us, length us, event | category | flops | bytes accessed | tf_op | source)
XLA Modules:
  0.0 512.8 jit_solution(5501305438793525802)
XLA Ops:
  8.0 3.2 copy.151
  17.7 38.3 %all_to_all.39 = bf16[128,16,8,64]{0,3,1,2:T(8,128)(2,1)} all-to-all(bf16[128,16,8,64]{0,3,1,2:T(8,128)(2,1)S(1)} %copy.152), channel_id=1, replica_groups=mesh['blk'=16,'seq'=8] {'seq'}, dimensions={2} | all-to-all | bytes 4194304 | tf_op jit(solution)/shard_map/all_to_all | solution.py:42
  56.0 8.3 %all-gather.4.cloned.1.call-done = bf16[1024,1024]{1,0:T(8,128)(2,1)} async-done(((bf16[64,1024]{1,0:T(8,128)(2,1)}), bf16[1024,1024]{1,0:T(8,128)(2,1)}) %all-gather.4.cloned.1.call-update) | async-done | bytes 2097168 | tf_op jit(solution)/shard_map/all_gather | solution.py:45
  64.3 4.6 fusion.22
  68.9 55.1 %all_to_all.40 = f32[8,128,1024]{2,1,0:T(8,128)} all-to-all(f32[8,128,1024]{2,1,0:T(8,128)S(1)} %fusion.22), channel_id=1, replica_groups=mesh['blk'=16,'seq'=8] {'seq'}, dimensions={0} | all-to-all | bytes 8388608 | tf_op jit(solution)/shard_map/all_to_all | solution.py:18
  124.1 3.4 reduce_sum.66
  131.0 17.1 %all-gather = s32[1,1024]{1,0:T(1,128)S(1)} all-gather(s32[1,128]{1,0:T(1,128)S(1)} %copy-done.8), channel_id=2, replica_groups=mesh['blk'=16,'seq'=8] {'seq'}, dimensions={1}, use_global_device_ids=true | all-gather | bytes 4608 | tf_op jit(solution)/shard_map/all_gather | solution.py:70
  148.3 30.2 %all-gather.6.cloned.1.call-done = bf16[1024,1024]{1,0:T(8,128)(2,1)} async-done(((bf16[128,1024]{1,0:T(8,128)(2,1)}), bf16[1024,1024]{1,0:T(8,128)(2,1)}) %all-gather.6.cloned.1.call-update) | async-done | bytes 2097168 | tf_op jit(solution)/shard_map/all_gather | solution.py:69
  183.0 9.1 %fusion.33 = (f32[4,8,128]{2,1,0:T(8,128)S(1)}, f32[4,8,128,1024]{2,3,1,0:T(8,128)}) fusion(bf16[1024,4,128,1]{0,2,3,1:T(8,128)(2,1)S(1)} %bitcast.123, bf16[128,4,8,128]{3,2,1,0:T(8,128)(2,1)} %bitcast.125, pred[128,1024]{0,1:T(8,128)(4,1)S(1)} %fusion.29), kind=kOutput, calls=%fused_computation.52 | convolution fusion | flops 1086320640 | bytes 19021824 | tf_op jit(solution)/shard_map/qgjd,kgd->gjqk/dot_general | solution.py:55
  194.4 8.7 %fusion.1 = f32[4,8,128]{2,1,0:T(8,128)S(1)} fusion(f32[4,8,128,1024]{2,3,1,0:T(8,128)} %get-tuple-element.45, f32[4,8,128]{2,1,0:T(8,128)S(1)} %broadcast_maximum_fusion, pred[128,1024]{0,1:T(8,128)(4,1)S(1)} %fusion.29), kind=kLoop, calls=%fused_computation.5 | loop fusion | flops 12578816 | bytes 16941056 | tf_op jit(solution)/shard_map/reduce_sum | solution.py:78
  203.1 9.9 %fusion.21 = (bf16[128,4,8,128]{0,3,2,1:T(8,128)(2,1)}, f32[4,8,128,128]{2,3,1,0:T(8,128)S(1)}) fusion(f32[128,4,8]{0,2,1:T(8,128)S(1)} %bitcast.141, bf16[1024,4,128,1]{0,2,3,1:T(8,128)(2,1)S(1)} %bitcast.139, f32[4,8,128,1024]{2,3,1,0:T(8,128)} %get-tuple-element.45, f32[4,8,128]{2,1,0:T(8,128)S(1)} %broadcast_maximum_fusion, ...), kind=kOutput, calls=%fused_computation.32 | convolution fusion | flops 1087373312 | bytes 21135360 | tf_op jit(solution)/shard_map/gjqk,kgd->gjqd/dot_general | solution.py:77
  213.4 9.5 %fusion.24 = f32[1024,4,128]{2,0,1:T(8,128)} fusion(bf16[4,8,128,128]{2,3,1,0:T(8,128)(2,1)S(1)} %bitcast.132, f32[4,8,128,1024]{2,3,1,0:T(8,128)} %get-tuple-element.45, f32[4,8,128]{2,1,0:T(8,128)S(1)} %log_add_fusion, pred[128,1024]{0,1:T(8,128)(4,1)S(1)} %fusion.29), kind=kOutput, calls=%fused_computation.39 | convolution fusion | flops 1086324736 | bytes 20070400 | tf_op jit(solution)/shard_map/gjqk,gjqd->kgd/dot_general | solution.py:96
  222.9 10.9 %fusion = bf16[4,8,128,1024]{2,3,1,0:T(8,128)(2,1)} fusion(f32[4,8,128,1024]{2,3,1,0:T(8,128)} %get-tuple-element.45, bf16[1024,4,128,1]{0,2,3,1:T(8,128)(2,1)S(1)} %bitcast.140, bf16[4,8,128,128]{2,3,1,0:T(8,128)(2,1)S(1)} %bitcast.133, f32[4,8,128]{2,1,0:T(8,128)S(1)} %multiply_reduce_fusion.3, f32[4,8,128]{2,1,0:T(8,128)S(1)} %log_add_fusion, ...), kind=kOutput, calls=%fused_computation.1 | convolution fusion | flops 1094713344 | bytes 27426816 | tf_op jit(solution)/shard_map/gjqd,kgd->gjqk/dot_general | solution.py:93
  236.7 3.5 copy.198
  240.1 7.1 %fusion.20 = f32[1024,4,128]{2,0,1:T(8,128)} fusion(bf16[4,8,128,1024]{2,3,1,0:T(8,128)(2,1)} %fusion, bf16[128,4,8,128]{3,2,1,0:T(8,128)(2,1)S(1)} %bitcast.126), kind=kOutput, calls=%fused_computation.30 | convolution fusion | flops 1074266112 | bytes 11534336 | tf_op jit(solution)/shard_map/gjqk,qgjd->kgd/dot_general | solution.py:98
  253.4 50.9 %all_to_all.41 = f32[8,128,1024]{1,2,0:T(8,128)} all-to-all(f32[8,128,1024]{1,2,0:T(8,128)S(1)} %copy.167), channel_id=1, replica_groups=mesh['blk'=16,'seq'=8] {'seq'}, dimensions={0} | all-to-all | bytes 8388608 | tf_op jit(solution)/shard_map/all_to_all | solution.py:18
  310.2 4.3 all-to-all-start.3
  314.7 4.7 copy.175
  319.4 22.8 %all-to-all-done.3 = bf16[8,128,1024]{2,1,0:T(8,128)(2,1)} async-done(((bf16[8,128,1024]{2,1,0:T(8,128)(2,1)}), bf16[8,128,1024]{2,1,0:T(8,128)(2,1)}, u32[]{:S(2)}, u32[]{:S(2)}) %all-to-all-start.3) | async-done | bytes 2097184 | tf_op jit(solution)/shard_map/all_to_all | solution.py:112
  342.2 6.5 %fusion.17 = f32[1024,1024]{1,0:T(8,128)} fusion(bf16[1024,1024]{1,0:T(8,128)(2,1)} %bitcast.31, bf16[128,8,8,128]{3,2,1,0:T(8,128)(2,1)} %bitcast.136), kind=kOutput, calls=%fused_computation.26 | convolution fusion | flops 2147483648 | bytes 8388608 | tf_op jit(solution)/shard_map/dot_general | solution.py:116
  348.7 5.9 %convolution_convert_fusion = bf16[1024,1024]{0,1:T(8,128)(2,1)} fusion(bf16[1024,1024]{1,0:T(8,128)(2,1)} %bitcast.31, bf16[1024,1024]{1,0:T(8,128)(2,1)} %all-gather.4.cloned.1.call-done), kind=kOutput, calls=%fused_computation.38 | convolution fusion | flops 2148532224 | bytes 6291456 | tf_op jit(solution)/shard_map/dot_general | solution.py:121
  354.6 6.2 %copy.170 = bf16[1024,16,1,64]{3,1,2,0:T(8,128)(2,1)} copy(bf16[1024,16,1,64]{0,3,1,2:T(8,128)(2,1)} %bitcast.135) | data formatting | bytes 4194304 | tf_op jit(solution)/shard_map/reshape | solution.py:124
  360.8 7.6 %reshape.229 = bf16[8,2,65536]{2,1,0:T(2,128)(2,1)} reshape(bf16[1024,1,16,64]{3,2,1,0:T(8,128)(2,1)} %bitcast.120) | data formatting | bytes 4194304
  368.4 4.6 all-to-all-start.4
  376.3 5.7 %multiply_convert_fusion.1 = bf16[4,128,8,128]{3,1,2,0:T(8,128)(2,1)} fusion(bf16[1024,4,128,1]{0,2,3,1:T(8,128)(2,1)S(1)} %bitcast.124, bf16[4,8,128,1024]{2,3,1,0:T(8,128)(2,1)} %fusion), kind=kOutput, calls=%fused_computation.35 | convolution fusion | flops 1074790400 | bytes 10485760 | tf_op jit(solution)/shard_map/gjqk,kgd->qgjd/dot_general | solution.py:102
  384.2 22.7 %all-to-all-done.4 = bf16[8,2,65536]{2,1,0:T(2,128)(2,1)} async-done(((bf16[8,2,65536]{2,1,0:T(2,128)(2,1)}), bf16[8,2,65536]{2,1,0:T(2,128)(2,1)}, u32[]{:S(2)}, u32[]{:S(2)}) %all-to-all-start.4) | async-done | bytes 2097184 | tf_op jit(solution)/shard_map/all_to_all | solution.py:125
  406.9 7.4 %reshape.230 = bf16[1024,1,16,64]{3,2,1,0:T(8,128)(2,1)} reshape(bf16[8,2,65536]{2,1,0:T(2,128)(2,1)} %all-to-all-done.4) | data formatting | bytes 4194304
  414.3 5.5 %copy.171 = bf16[1024,16,1,64]{0,3,2,1:T(8,128)(2,1)} copy(bf16[1024,16,1,64]{3,1,2,0:T(8,128)(2,1)} %bitcast.121) | data formatting | bytes 4194304 | tf_op jit(solution)/shard_map/all_to_all | solution.py:125
  425.2 4.8 multiply_reduce_fusion
  430.0 4.4 fusion.16
  434.4 4.1 copy.179
  438.7 67.3 %psum.7 = f32[8192]{0:T(1024)} all-reduce(f32[8192]{0:T(1024)S(1)} %reduce_sum.72), channel_id=1, replica_groups=mesh['blk'=16,'seq'=8] {'blk','seq'}, use_global_device_ids=true, to_apply=%region_9.10 | all-reduce | flops 8192 | bytes 65536 | tf_op jit(solution)/shard_map/psum | solution.py:129
  (58 shorter events, 44.5 us)
Async XLA Ops:
  7.2 57.1 %all-gather.4.cloned.1.call-start = ((), (), s32[]{:S(2)}) async-start(), calls=%async_computation.6 | async-start | bytes 2228224 | tf_op jit(solution)/shard_map/all_gather | solution.py:45
  7.9 5.5 %copy-start.7 = (f32[8192]{0:T(1024)S(1)}, f32[8192]{0:T(1024)}, u32[]{:S(2)}) copy-start(f32[8192]{0:T(1024)} %param.11) | copy-start | bytes 98308
  7.9 170.6 %all-gather.6.cloned.1.call-start = ((), (), s32[]{:S(2)}) async-start(), calls=%async_computation.7 | async-start | bytes 2359296 | tf_op jit(solution)/shard_map/all_gather | solution.py:69
  124.0 3.5 copy-start.5
  124.0 6.9 %copy-start.8 = (s32[1,128]{1,0:T(1,128)S(1)}, s32[1,128]{1,0:T(1,128)}, u32[]{:S(2)}) copy-start(s32[1,128]{1,0:T(1,128)} %param.9) | copy-start | bytes 1540
  194.4 8.7 %copy-start.6 = (bf16[1024,512]{0,1:T(8,128)(2,1)S(1)}, bf16[1024,512]{0,1:T(8,128)(2,1)}, u32[]{:S(2)}) copy-start(bf16[1024,512]{0,1:T(8,128)(2,1)} %copy.157) | copy-start | bytes 3145732
  203.1 9.9 %copy-start.3 = (bf16[1,128,4096]{1,2,0:T(8,128)(2,1)S(1)}, bf16[1,128,4096]{1,2,0:T(8,128)(2,1)}, u32[]{:S(2)}) copy-start(bf16[1,128,4096]{1,2,0:T(8,128)(2,1)} %copy.159) | copy-start | bytes 3145732
  236.7 3.5 copy-start.1
  250.1 2.2 copy-start.2
  310.2 32.0 %all-to-all-start.3 = ((bf16[8,128,1024]{2,1,0:T(8,128)(2,1)}), bf16[8,128,1024]{2,1,0:T(8,128)(2,1)}, u32[]{:S(2)}, u32[]{:S(2)}) async-start(bf16[8,128,1024]{2,1,0:T(8,128)(2,1)} %stack.2), calls=%async_computation.3 | async-start | bytes 4194304 | tf_op jit(solution)/shard_map/all_to_all | solution.py:112
  314.5 191.5 %reduce-scatter.2.cloned.1.call-start = ((), (), s32[]{:S(2)}) async-start(), calls=%async_computation.8 | async-start | bytes 4456448 | tf_op jit(solution)/shard_map/reduce_scatter | solution.py:115
  368.4 38.6 %all-to-all-start.4 = ((bf16[8,2,65536]{2,1,0:T(2,128)(2,1)}), bf16[8,2,65536]{2,1,0:T(2,128)(2,1)}, u32[]{:S(2)}, u32[]{:S(2)}) async-start(bf16[8,2,65536]{2,1,0:T(2,128)(2,1)} %reshape.229), calls=%async_computation.4 | async-start | bytes 4194304 | tf_op jit(solution)/shard_map/all_to_all | solution.py:125
  422.9 2.2 copy-start
  422.9 2.3 copy-start.4
Sparse Core Ops, SparseCore 0:
  9.7 54.5 all-gather.3
  127.6 50.8 all-gather.5
  348.8 70.4 reduce-scatter.1
